TPU v7x, 16 devices: a 4x2x1 block of a 4x4x8 slice. The times are simulated.
16 devices in a mesh: rep: 2 (over y, z), dp: 8 (over x, core).
Axes of the slice: x: 4, y: 2, z: 1, core: 2. Of those that a mesh axis runs over, the one named last changes fastest.
The devices are a block of a 4x4x8 slice.
Arguments:
- x: bfloat16 [16, 2048, 512], P(('rep', 'dp')), parts along dimension 0
- dy: bfloat16 [16, 2048, 512], P(('rep', 'dp')), parts along dimension 0
- w_gate: bfloat16 [2, 512, 2048], replicated
- w_up: bfloat16 [2, 512, 2048], replicated
- w_down: bfloat16 [2, 2048, 512], replicated
- m_w_gate: float32 [2, 512, 2048], replicated
- m_w_up: float32 [2, 512, 2048], replicated
- m_w_down: float32 [2, 2048, 512], replicated
- v_w_gate: float32 [2, 512, 2048], replicated
- v_w_up: float32 [2, 512, 2048], replicated
- v_w_down: float32 [2, 2048, 512], replicated
Outputs:
- output 1: bfloat16 [4, 512, 2048], P('rep'), parts along dimension 0
- output 2: bfloat16 [4, 512, 2048], P('rep'), parts along dimension 0
- output 3: bfloat16 [4, 2048, 512], P('rep'), parts along dimension 0
- output 4: float32 [4, 512, 2048], P('rep'), parts along dimension 0
- output 5: float32 [4, 512, 2048], P('rep'), parts along dimension 0
- output 6: float32 [4, 2048, 512], P('rep'), parts along dimension 0
- output 7: float32 [4, 512, 2048], P('rep'), parts along dimension 0
- output 8: float32 [4, 512, 2048], P('rep'), parts along dimension 0
- output 9: float32 [4, 2048, 512], P('rep'), parts along dimension 0
There are 2 independent parts. A program takes and returns all parts, laid end to end along the dimension named above; an argument that names none is the same for every part.
All inputs are finite; a program needn't handle non-finite values.
Results may differ from a plain program's by a relative error of at most 0.02.
Values are sent between devices in bfloat16 or wider.
A program may use at most 768 MiB of HBM per device.

v0:
```python
import jax
import jax.numpy as jnp
from jax import lax
from jax.sharding import PartitionSpec as P

NAMES = ("w_gate", "w_up", "w_down")


def matmul(a, w):
    return jnp.dot(a, w, preferred_element_type=jnp.float32).astype(jnp.bfloat16)


def normed(h):
    wide = h.astype(jnp.float32)
    scale = lax.rsqrt(jnp.mean(wide**2, -1, keepdims=True) + 1e-6)
    return (wide * scale).astype(jnp.bfloat16)


def layer(h, w):
    a = normed(h)
    gate = jnp.dot(a, w["w_gate"], preferred_element_type=jnp.float32)
    up = jnp.dot(a, w["w_up"], preferred_element_type=jnp.float32)
    return h + matmul((jax.nn.silu(gate) * up).astype(jnp.bfloat16), w["w_down"])


def adamw(w, m, v, g):
    m = 0.9 * m + 0.1 * g
    v = 0.95 * v + 0.05 * g * g
    step = m * lax.rsqrt(v + 1e-8) + 0.1 * w
    return (w - 0.02 * step).astype(jnp.bfloat16), m, v


def solution(mesh):
    def step(x, dy, *arrays):
        weights, m, v = (arrays[i : i + 3] for i in (0, 3, 6))
        layers = weights[0].shape[0]
        h, kept = x[0], []
        for number in range(layers):
            kept.append(h)
            h = layer(h, {name: w[number] for name, w in zip(NAMES, weights, strict=True)})
        by_h, summed = dy[0], [None] * layers
        for number in reversed(range(layers)):
            _, back = jax.vjp(lambda w, h: layer(h, w), {name: w[number] for name, w in zip(NAMES, weights, strict=True)}, kept[number])
            by_w, by_h = back(by_h)
            summed[number] = [lax.psum(by_w[name], "dp") for name in NAMES]
        gradients = [jnp.stack([summed[number][i] for number in range(layers)]).astype(jnp.float32) for i in range(3)]
        new = [adamw(w.astype(jnp.float32), m, v, g) for w, m, v, g in zip(weights, m, v, gradients, strict=True)]
        return tuple(one[which] for which in range(3) for one in new)

    return jax.shard_map(
        step,
        mesh=mesh,
        in_specs=(P(("rep", "dp"), None, None),) * 2 + (P(None, None, None),) * 9,
        out_specs=(P("rep", None, None),) * 9,
        check_vma=False,
    )
```

profile of v0, /device:TPU:112, one launch (start us, length us, event | category | flops | bytes accessed | tf_op | source)
XLA Modules:
  0.0 387.1 jit_solution(5613051811933247367)
XLA Ops:
  7.2 0.1 all-reduce.3.cloned.1.call-start
  7.3 2.9 copy.20
  10.2 0.5 fusion.30
  10.7 4.2 %copy.21 = bf16[1,2048,512]{1,2,0:T(8,128)(2,1)} copy(bf16[1,2048,512]{2,1,0:T(8,128)(2,1)} %param.12) | data formatting | bytes 4194304 | tf_op args[1]
  14.9 10.3 %convolution_convert_fusion.1 = bf16[2048,2048]{1,0:T(8,128)(2,1)} fusion(bf16[1,2048,512]{2,1,0:T(8,128)(2,1)} %param.12, bf16[2,2048,512]{2,1,0:T(8,128)(2,1)} %param.15), kind=kOutput, calls=%fused_computation.52 | convolution fusion | flops 4299161600 | bytes 12582912 | tf_op jit(solution)/shard_map/transpose(jvp())/dot_general | solution.py:10
  25.2 8.2 %fusion.70 = f32[2048,2048]{1,0:T(8,128)} fusion(bf16[2,512,2048]{2,1,0:T(8,128)(2,1)S(1)} %copy-done.3, bf16[1,2048,512]{2,1,0:T(8,128)(2,1)S(1)} %copy-done.10, f32[2048]{0:T(1024)S(1)} %add_rsqrt_fusion), kind=kOutput, calls=%fused_computation.103 | convolution fusion | flops 4298113024 | bytes 20979712 | tf_op jit(solution)/shard_map/dot_general | solution.py:21
  33.4 17.7 %multiply_convert_fusion.1 = (bf16[2048,2048]{1,0:T(8,128)(2,1)}, f32[2048,2048]{1,0:T(8,128)}) fusion(f32[2048,2048]{1,0:T(8,128)} %fusion.70, bf16[2,512,2048]{2,1,0:T(8,128)(2,1)} %param.14, bf16[1,2048,512]{2,1,0:T(8,128)(2,1)S(1)} %copy-done.10, f32[2048]{0:T(1024)S(1)} %add_rsqrt_fusion), kind=kOutput, calls=%fused_computation.17 | convolution fusion | flops 4323278848 | bytes 46145536 | tf_op jit(solution)/shard_map/dot_general | solution.py:22
  51.1 9.1 %fusion.34 = (f32[2048]{0:T(1024)S(1)}, bf16[2048,512]{0,1:T(8,128)(2,1)S(1)}) fusion(bf16[2048,2048]{1,0:T(8,128)(2,1)} %get-tuple-element.24, bf16[2,2048,512]{2,1,0:T(8,128)(2,1)} %param.15, bf16[1,2048,512]{1,2,0:T(8,128)(2,1)S(1)} %copy.20), kind=kOutput, calls=%fused_computation.64 | convolution fusion | flops 4300208128 | bytes 14688256 | tf_op jit(solution)/shard_map/dot_general | solution.py:10
  60.3 1.3 copy-done.12
  61.5 8.3 %fusion.59 = f32[2048,2048]{1,0:T(8,128)} fusion(bf16[2,512,2048]{2,1,0:T(8,128)(2,1)S(1)} %copy-done.6, bf16[2048,512]{0,1:T(8,128)(2,1)S(1)} %get-tuple-element.27, f32[2048]{0:T(1024)S(1)} %fusion.89), kind=kOutput, calls=%fused_computation.92 | convolution fusion | flops 4298113024 | bytes 20979712 | tf_op jit(solution)/shard_map/jvp()/dot_general | solution.py:22
  69.8 22.9 %fusion.2 = (bf16[2048,2048]{1,0:T(8,128)(2,1)}, f32[2048,2048]{1,0:T(8,128)}) fusion(f32[2048,2048]{1,0:T(8,128)} %fusion.59, bf16[2048,2048]{1,0:T(8,128)(2,1)} %convolution_convert_fusion.1, bf16[2,512,2048]{2,1,0:T(8,128)(2,1)} %param.13, bf16[2048,512]{0,1:T(8,128)(2,1)} %copy-done.12, f32[2048]{0:T(1024)S(1)} %fusion.89), kind=kOutput, calls=%fused_computation.8 | convolution fusion | flops 4348444672 | bytes 54534144 | tf_op jit(solution)/shard_map/jvp()/dot_general | solution.py:21
  92.8 14.5 %fusion.49 = bf16[1,2048,512]{2,1,0:T(8,128)(2,1)} fusion(f32[2048,2048]{1,0:T(8,128)} %fusion.59, bf16[1,2048,512]{2,1,0:T(8,128)(2,1)S(1)} %copy-done.11, f32[2048,2048]{1,0:T(8,128)} %get-tuple-element.29), kind=kOutput, calls=%fused_computation.84 | convolution fusion | flops 4321181696 | bytes 37748736 | tf_op jit(solution)/shard_map/transpose(jvp())/dot_general | solution.py:10
  107.2 12.4 %fusion.48 = bf16[1,512,2048]{2,1,0:T(8,128)(2,1)} fusion(bf16[2048,2048]{1,0:T(8,128)(2,1)} %convolution_convert_fusion.1, bf16[2048,512]{0,1:T(8,128)(2,1)S(1)} %copy-done.13, f32[2048]{0:T(1024)S(1)} %fusion.89, f32[2048,2048]{1,0:T(8,128)} %get-tuple-element.29), kind=kOutput, calls=%fused_computation.83 | convolution fusion | flops 4324327424 | bytes 29368320 | tf_op jit(solution)/shard_map/transpose(jvp())/dot_general | solution.py:22
  119.6 11.4 %fusion.41 = bf16[2048,512]{0,1:T(8,128)(2,1)S(1)} fusion(bf16[2048,2048]{1,0:T(8,128)(2,1)} %convolution_convert_fusion.1, bf16[2,512,2048]{2,1,0:T(8,128)(2,1)S(1)} %copy-done.7, f32[2048,2048]{1,0:T(8,128)} %get-tuple-element.29), kind=kOutput, calls=%fused_computation.75 | convolution fusion | flops 4321181696 | bytes 29360128 | tf_op jit(solution)/shard_map/transpose(jvp())/dot_general | solution.py:22
  131.0 9.3 %fusion.46 = bf16[1,512,2048]{2,1,0:T(8,128)(2,1)} fusion(bf16[2048,2048]{1,0:T(8,128)(2,1)} %get-tuple-element.28, bf16[2048,512]{0,1:T(8,128)(2,1)S(1)} %copy-done.13, f32[2048]{0:T(1024)S(1)} %fusion.89), kind=kOutput, calls=%fused_computation.81 | convolution fusion | flops 4298113024 | bytes 12591104 | tf_op jit(solution)/shard_map/transpose(jvp())/dot_general | solution.py:21
  140.3 9.0 %fusion.36 = (f32[2048]{0:T(1024)S(1)}, bf16[2048,512]{0,1:T(8,128)(2,1)S(1)}) fusion(bf16[2048,512]{0,1:T(8,128)(2,1)S(1)} %copy-done.13, bf16[2048,512]{0,1:T(8,128)(2,1)S(1)} %fusion.41, bf16[2048,2048]{1,0:T(8,128)(2,1)} %get-tuple-element.28, bf16[2,512,2048]{2,1,0:T(8,128)(2,1)S(1)} %copy-done.4), kind=kOutput, calls=%fused_computation.66 | convolution fusion | flops 4300208128 | bytes 16785408 | tf_op jit(solution)/shard_map/transpose(jvp())/dot_general | solution.py:21
  149.3 1.4 fusion.56
  150.7 9.7 %fusion.45 = bf16[1,2048,512]{2,1,0:T(8,128)(2,1)} fusion(bf16[2048,2048]{1,0:T(8,128)(2,1)} %get-tuple-element.24, bf16[2048,512]{0,1:T(8,128)(2,1)S(1)} %fusion.56), kind=kOutput, calls=%fused_computation.80 | convolution fusion | flops 4296015872 | bytes 12582912 | tf_op jit(solution)/shard_map/transpose(jvp())/dot_general | solution.py:10
  160.4 5.1 %convolution_convert_fusion = bf16[2048,2048]{1,0:T(8,128)(2,1)S(1)} fusion(bf16[2048,512]{0,1:T(8,128)(2,1)S(1)} %fusion.56, bf16[2,2048,512]{2,1,0:T(8,128)(2,1)S(1)} %copy-done.9), kind=kOutput, calls=%fused_computation.51 | convolution fusion | flops 4299161600 | bytes 12582912 | tf_op jit(solution)/shard_map/transpose(jvp())/dot_general | solution.py:10
  165.6 13.5 %fusion.47 = bf16[1,512,2048]{2,1,0:T(8,128)(2,1)} fusion(bf16[2048,2048]{1,0:T(8,128)(2,1)S(1)} %convolution_convert_fusion, f32[2048,2048]{1,0:T(8,128)} %fusion.70, bf16[1,2048,512]{1,2,0:T(8,128)(2,1)S(1)} %copy-done.1, f32[2048]{0:T(1024)S(1)} %copy-done.17), kind=kOutput, calls=%fused_computation.82 | convolution fusion | flops 4324327424 | bytes 29368320 | tf_op jit(solution)/shard_map/transpose(jvp())/dot_general | solution.py:22
  179.1 17.6 %fusion.50 = bf16[1,512,2048]{2,1,0:T(8,128)(2,1)} fusion(f32[2048,2048]{1,0:T(8,128)} %fusion.70, f32[2048,2048]{1,0:T(8,128)} %get-tuple-element.25, bf16[2048,2048]{1,0:T(8,128)(2,1)} %copy-done.18, bf16[1,2048,512]{1,2,0:T(8,128)(2,1)S(1)} %copy-done.1, f32[2048]{0:T(1024)S(1)} %copy-done.17), kind=kOutput, calls=%fused_computation.85 | convolution fusion | flops 4345298944 | bytes 46145536 | tf_op jit(solution)/shard_map/transpose(jvp())/dot_general | solution.py:21
  196.7 138.6 %all-reduce.3.cloned.1.call-done = (bf16[1,512,2048]{2,1,0:T(8,128)(2,1)}, bf16[1,512,2048]{2,1,0:T(8,128)(2,1)}, bf16[1,512,2048]{2,1,0:T(8,128)(2,1)}, bf16[1,...) async-done(((bf16[1,512,2048]{2,1,0:T(8,128)(2,1)}, bf16[1,512,2048]{2,1,0:T(8,128)(2,1)}, bf16[1,512,2048]{2,1,0:T(8,128)(2,1)}, ...) | async-done | bytes 12582928 | tf_op jit(solution)/shard_map/psum | solution.py:45
  335.3 16.7 %fusion.23 = (bf16[2,2048,512]{2,1,0:T(8,128)(2,1)}, f32[2,2048,512]{2,1,0:T(8,128)}, f32[2,2048,512]{2,1,0:T(8,128)}) fusion(bf16[2,2048,512]{2,1,0:T(8,128)(2,1)} %param.15, bf16[1,2048,512]{2,1,0:T(8,128)(2,1)} %get-tuple-element.13, bf16[1,2048,512]{2,1,0:T(8,128)(2,1)} %get-tuple-element.14, f32[2,2048,512]{2,1,0:T(8,128)} %param.21, ...), kind=kLoop, calls=%fused_computation.44 | loop fusion | flops 39845888 | bytes 46137344 | tf_op jit(solution)/shard_map/convert_element_type | solution.py:30
  352.0 27.7 %fusion.15 = (bf16[2,512,2048]{2,1,0:T(8,128)(2,1)}, f32[2,512,2048]{2,1,0:T(8,128)}, f32[2,512,2048]{2,1,0:T(8,128)}, bf16[2,512,2048]{2,1,0:T(8,128)(2,1)}, f3...) fusion(bf16[2,512,2048]{2,1,0:T(8,128)(2,1)S(1)} %copy-done.5, bf16[1,512,2048]{2,1,0:T(8,128)(2,1)} %get-tuple-element.9, ...), kind=kLoop, calls=%fused_computation.36 | loop fusion | flops 79691776 | bytes 92274688 | tf_op jit(solution)/shard_map/convert_element_type | solution.py:30
  (41 shorter events, 0.2 us)
Async XLA Ops:
  7.2 328.2 %all-reduce.3.cloned.1.call-start = ((), (), s32[]{:S(2)}) async-start(), calls=%async_computation | async-start | bytes 25165824 | tf_op jit(solution)/shard_map/psum | solution.py:45
  10.2 40.9 %copy-start = (bf16[1,2048,512]{1,2,0:T(8,128)(2,1)}, bf16[1,2048,512]{1,2,0:T(8,128)(2,1)S(1)}, u32[]{:S(2)}) copy-start(bf16[1,2048,512]{1,2,0:T(8,128)(2,1)S(1)} %copy.20) | copy-start | bytes 6291460
  10.7 22.7 %copy-start.16 = (f32[2048]{0:T(1024)}, f32[2048]{0:T(1024)S(1)}, u32[]{:S(2)}) copy-start(f32[2048]{0:T(1024)S(1)} %add_rsqrt_fusion) | copy-start | bytes 24580
  14.8 10.3 %copy-start.3 = (bf16[2,512,2048]{2,1,0:T(8,128)(2,1)S(1)}, bf16[2,512,2048]{2,1,0:T(8,128)(2,1)}, u32[]{:S(2)}) copy-start(bf16[2,512,2048]{2,1,0:T(8,128)(2,1)} %param.13) | copy-start | bytes 12582916
  14.8 10.3 %copy-start.10 = (bf16[1,2048,512]{2,1,0:T(8,128)(2,1)S(1)}, bf16[1,2048,512]{2,1,0:T(8,128)(2,1)}, u32[]{:S(2)}) copy-start(bf16[1,2048,512]{2,1,0:T(8,128)(2,1)} %param.11) | copy-start | bytes 6291460
  51.1 10.4 %copy-start.6 = (bf16[2,512,2048]{2,1,0:T(8,128)(2,1)S(1)}, bf16[2,512,2048]{2,1,0:T(8,128)(2,1)}, u32[]{:S(2)}) copy-start(bf16[2,512,2048]{2,1,0:T(8,128)(2,1)} %param.14) | copy-start | bytes 12582916
  60.2 1.3 copy-start.12
  60.2 1.3 copy-start.14
  69.8 22.9 %copy-start.11 = (bf16[1,2048,512]{2,1,0:T(8,128)(2,1)S(1)}, bf16[1,2048,512]{2,1,0:T(8,128)(2,1)}, u32[]{:S(2)}) copy-start(bf16[1,2048,512]{2,1,0:T(8,128)(2,1)} %param.12) | copy-start | bytes 6291460
  92.7 14.5 %copy-start.13 = (bf16[2048,512]{0,1:T(8,128)(2,1)S(1)}, bf16[2048,512]{0,1:T(8,128)(2,1)}, u32[]{:S(2)}) copy-start(bf16[2048,512]{0,1:T(8,128)(2,1)} %copy-done.12) | copy-start | bytes 6291460
  107.2 12.4 %copy-start.7 = (bf16[2,512,2048]{2,1,0:T(8,128)(2,1)S(1)}, bf16[2,512,2048]{2,1,0:T(8,128)(2,1)}, u32[]{:S(2)}) copy-start(bf16[2,512,2048]{2,1,0:T(8,128)(2,1)} %param.14) | copy-start | bytes 12582916
  131.0 9.3 %copy-start.4 = (bf16[2,512,2048]{2,1,0:T(8,128)(2,1)S(1)}, bf16[2,512,2048]{2,1,0:T(8,128)(2,1)}, u32[]{:S(2)}) copy-start(bf16[2,512,2048]{2,1,0:T(8,128)(2,1)} %param.13) | copy-start | bytes 12582916
  140.2 9.0 %copy-start.15 = (f32[2048]{0:T(1024)S(1)}, f32[2048]{0:T(1024)}, u32[]{:S(2)}) copy-start(f32[2048]{0:T(1024)} %copy-done.14) | copy-start | bytes 24580
  140.2 9.1 %copy-start.2 = (bf16[1,2048,512]{1,2,0:T(8,128)(2,1)S(1)}, bf16[1,2048,512]{1,2,0:T(8,128)(2,1)}, u32[]{:S(2)}) copy-start(bf16[1,2048,512]{1,2,0:T(8,128)(2,1)} %copy.21) | copy-start | bytes 6291460
  150.7 9.7 %copy-start.9 = (bf16[2,2048,512]{2,1,0:T(8,128)(2,1)S(1)}, bf16[2,2048,512]{2,1,0:T(8,128)(2,1)}, u32[]{:S(2)}) copy-start(bf16[2,2048,512]{2,1,0:T(8,128)(2,1)} %param.15) | copy-start | bytes 12582916
  160.4 5.1 %copy-start.1 = (bf16[1,2048,512]{1,2,0:T(8,128)(2,1)S(1)}, bf16[1,2048,512]{1,2,0:T(8,128)(2,1)}, u32[]{:S(2)}) copy-start(bf16[1,2048,512]{1,2,0:T(8,128)(2,1)} %copy-done) | copy-start | bytes 6291460
  160.4 5.1 %copy-start.17 = (f32[2048]{0:T(1024)S(1)}, f32[2048]{0:T(1024)}, u32[]{:S(2)}) copy-start(f32[2048]{0:T(1024)} %copy-done.16) | copy-start | bytes 24580
  165.6 13.5 %copy-start.18 = (bf16[2048,2048]{1,0:T(8,128)(2,1)}, bf16[2048,2048]{1,0:T(8,128)(2,1)S(1)}, u32[]{:S(2)}) copy-start(bf16[2048,2048]{1,0:T(8,128)(2,1)S(1)} %convolution_convert_fusion) | copy-start | bytes 25165828
  335.3 16.7 %copy-start.5 = (bf16[2,512,2048]{2,1,0:T(8,128)(2,1)S(1)}, bf16[2,512,2048]{2,1,0:T(8,128)(2,1)}, u32[]{:S(2)}) copy-start(bf16[2,512,2048]{2,1,0:T(8,128)(2,1)} %param.13) | copy-start | bytes 12582916
  335.3 16.7 %copy-start.8 = (bf16[2,512,2048]{2,1,0:T(8,128)(2,1)S(1)}, bf16[2,512,2048]{2,1,0:T(8,128)(2,1)}, u32[]{:S(2)}) copy-start(bf16[2,512,2048]{2,1,0:T(8,128)(2,1)} %param.14) | copy-start | bytes 12582916
Sparse Core Ops, SparseCore 0:
  196.8 138.4 all-reduce.2
where the time goes:
time: 394 us; the launch traced here: 387 us
  matrix products  179 us (45%)
  waiting for transfers between devices  139 us (35%)
  other arithmetic  46.2 us (12%)
  between operations  14.8 us (4%)
  local copies, waits for them, and re-layouts  8.49 us (2%)
    psum x1, waiting for transfers between devices, step(): summed[number] = [lax.psum(by_w[name], 'dp') for name in NAMES]  139 us
    dot_general x5, matrix products, layer(): gate = jnp.dot(a, w['w_gate'], preferred_element_type=jnp.float32)  67 us
    dot_general x5, matrix products, layer(): up = jnp.dot(a, w['w_up'], preferred_element_type=jnp.float32)  63.2 us
    dot_general x5, matrix products, matmul(): jnp.dot(a, w, preferred_element_type=jnp.float32).astype(jnp.bfloat16)  48.7 us
    convert_element_type x2, other arithmetic, adamw(): return ((w - 0.02 * step).astype(jnp.bfloat16), m, v)  44.4 us
    unnamed x40, local copies, waits for them, and re-layouts  8.49 us
  transfers between devices with their start and end apart: 1, of which 1 were waited for; matrix products, arithmetic and copies ran while one was open for 0% of the time, Pallas kernels for 0%

commit v1 on v0

v1 whole, which is shorter than its diff:
```python
import functools

import jax
import jax.numpy as jnp
from jax import lax
from jax.experimental import pallas as pl
from jax.experimental.pallas import tpu as pltpu
from jax.sharding import PartitionSpec as P

BF, F32 = jnp.bfloat16, jnp.float32
MESH = pl.DeviceIdType.MESH
VMEM_LIMIT = 64 * 1024 * 1024 - 256 * 1024


def dot(a, b):
    return lax.dot_general(a, b, (((1,), (0,)), ((), ())), preferred_element_type=F32)


def dot_t(a, b):
    return lax.dot_general(a, b, (((1,), (1,)), ((), ())), preferred_element_type=F32)


def norm(h):
    wide = h.astype(F32)
    scale = lax.rsqrt(jnp.mean(wide * wide, -1, keepdims=True) + 1e-6)
    return wide, scale, (wide * scale).astype(BF)


def chain_kernel(chunk, x_ref, dy_ref, wg, wu, wd, wide_out, turned, t1, t2):
    p2, dg2, du2, p1, dg1, du1 = (wide_out.at[i] for i in range(6))
    dyt, a2t, dh1t, a1t = (turned.at[i] for i in range(4))
    d = x_ref.shape[-1]
    chunks = wg.shape[-1] // chunk
    x = x_ref[...]
    _, _, a1 = norm(x)
    a1t[...] = a1.T
    down = None
    for c in range(chunks):
        cols = pl.ds(c * chunk, chunk)
        g = dot(a1, wg[0, :, cols])
        u = dot(a1, wu[0, :, cols])
        s = jax.nn.sigmoid(g)
        silu = g * s
        p = (silu * u).astype(BF)
        p1[c] = p
        t1[c] = silu
        t2[c] = u * (s * (1.0 + g * (1.0 - s)))
        term = dot(p, wd[0, cols, :])
        down = term if down is None else down + term
    h1 = x + down.astype(BF)
    wide, scale, a2 = norm(h1)
    a2t[...] = a2.T
    dy = dy_ref[...]
    dyt[...] = dy.T
    dag = dau = None
    for c in range(chunks):
        cols = pl.ds(c * chunk, chunk)
        g = dot(a2, wg[1, :, cols])
        u = dot(a2, wu[1, :, cols])
        dp = dot_t(dy, wd[1, cols, :]).astype(BF).astype(F32)
        s = jax.nn.sigmoid(g)
        silu = g * s
        p2[c] = (silu * u).astype(BF)
        du = (dp * silu).astype(BF)
        dg = (dp * (u * (s * (1.0 + g * (1.0 - s))))).astype(BF)
        du2[c] = du
        dg2[c] = dg
        tg = dot_t(dg, wg[1, :, cols])
        tu = dot_t(du, wu[1, :, cols])
        dag = tg if dag is None else dag + tg
        dau = tu if dau is None else dau + tu
    da = (dag.astype(BF) + dau.astype(BF)).astype(F32)
    dscale = jnp.sum(da * wide, -1, keepdims=True)
    dwide = da * scale - wide * (scale * scale * scale * dscale * (1.0 / d))
    dh1 = dy + dwide.astype(BF)
    dh1t[...] = dh1.T
    for c in range(chunks):
        cols = pl.ds(c * chunk, chunk)
        dp = dot_t(dh1, wd[0, cols, :]).astype(BF).astype(F32)
        du1[c] = (dp * t1[c]).astype(BF)
        dg1[c] = (dp * t2[c]).astype(BF)


def chain(x, dy, wg, wu, wd, tile=512, chunk=512):
    tokens, d = x.shape
    ff = wg.shape[-1]
    whole = lambda w: pl.BlockSpec(w.shape, lambda i: (0, 0, 0), pipeline_mode=pl.Buffered(1))
    rows = pl.BlockSpec((tile, d), lambda i: (i, 0))
    return pl.pallas_call(
        functools.partial(chain_kernel, chunk),
        name="chain",
        grid=(tokens // tile,),
        in_specs=[rows, rows, whole(wg), whole(wu), whole(wd)],
        out_specs=[
            pl.BlockSpec((6, ff // chunk, tile, chunk), lambda i: (0, 0, i, 0)),
            pl.BlockSpec((4, d, tile), lambda i: (0, 0, i)),
        ],
        out_shape=[jax.ShapeDtypeStruct((6, ff // chunk, tokens, chunk), BF), jax.ShapeDtypeStruct((4, d, tokens), BF)],
        scratch_shapes=[pltpu.VMEM((ff // chunk, tile, chunk), F32)] * 2,
        compiler_params=pltpu.CompilerParams(dimension_semantics=("arbitrary",), vmem_limit_bytes=VMEM_LIMIT),
    )(x, dy, wg, wu, wd)


def sum_kernel(n, wide, turned, out, g_ref, d_ref, i_ref, q_ref, go, left_op, right_op, *sems):
    (op_sem, out_sem, d_s, d_r, i_s, i_r, ii_s, ii_r, iii_s, iii_r, ag1_s, ag1_r, ag2_s, ag2_r, p_s, p_r) = sems
    mats, chunks = wide.shape[:2]
    pieces = g_ref.shape[1]
    half = pieces // 2
    per = pieces // chunks
    lanes = g_ref.shape[-1]
    me = lax.axis_index("dp")
    core = lax.rem(me, 2)
    chip = me // 2
    chips = n // 2
    partner = me + 1 - 2 * core
    chip_r = lax.rem(chip + 1, chips)
    chip_l = lax.rem(chip + chips - 1, chips)
    chip_o = lax.rem(chip + 2, chips)
    toward = (chip_r, chip_l)
    behind = (chip_l, chip_r)
    device = tuple(2 * c + core for c in toward)

    def piece(c, h):
        return core * half + 2 * c + h

    def remote(src, dst, s, r, to):
        return pltpu.make_async_remote_copy(src, dst, s, r, device_id={"dp": to}, device_id_type=MESH)

    def d_copy(k):
        return remote(g_ref.at[k, pl.ds((1 - core) * half, half)], d_ref.at[k], d_s.at[k], d_r.at[k], partner)

    def i_copy(k, e):
        return remote(g_ref.at[k, piece(chip_o, e)], i_ref.at[k, e], i_s.at[k, e], i_r.at[k, e], device[e])

    def ii_copy(k, e):
        return remote(g_ref.at[k, piece(toward[e], 1 - e)], q_ref.at[k, e, 1 - e], ii_s.at[k, e], ii_r.at[k, e], device[e])

    def iii_copy(k, e):
        return remote(i_ref.at[k, e], q_ref.at[k, e, e], iii_s.at[k, e], iii_r.at[k, e], device[e])

    def ag1_copy(k, e, c):
        span = go.at[k, pl.ds(piece(c, 0), 2)]
        return remote(span, span, ag1_s.at[k, e], ag1_r.at[k, e], device[e])

    def ag2_copy(k, e, c):
        span = go.at[k, piece(c, e)]
        return remote(span, span, ag2_s.at[k, e], ag2_r.at[k, e], device[e])

    def p_copy(k, j, c, owner):
        span = go.at[k, pl.ds(owner * half + 2 * c, 2)]
        return remote(span, span, p_s.at[k, j], p_r.at[k, j], partner)

    def left_load(k, slot):
        return pltpu.make_async_copy(turned.at[(2 * k + 1) // 3], left_op.at[slot], op_sem.at[slot])

    def right_load(t):
        k, c = t // chunks, lax.rem(t, chunks)
        c = lax.rem(c + (1 - core) * (chunks // 2), chunks)
        return pltpu.make_async_copy(wide.at[k, c], right_op.at[lax.rem(t, 3)], op_sem.at[2 + lax.rem(t, 3)])

    barrier = pltpu.get_barrier_semaphore()
    for to in (*device, partner):
        pl.semaphore_signal(barrier, inc=1, device_id={"dp": to}, device_id_type=MESH)
    left_load(0, 0).start()
    right_load(0).start()
    right_load(1).start()
    pl.semaphore_wait(barrier, 3)

    def multiply(k, c):
        t = k * chunks + c
        right_load(t).wait()

        @pl.when(t + 2 < mats * chunks)
        def _():
            right_load(t + 2).start()

        where = lax.rem(c + (1 - core) * (chunks // 2), chunks) * per
        a = left_op[lax.rem(k, 2)]
        for j in range(0, per, 2):
            b = right_op[lax.rem(t, 3), :, j * lanes : (j + 2) * lanes]
            block = dot(a, b).astype(BF)
            g_ref[k, where + j] = block[:, :lanes]
            g_ref[k, where + j + 1] = block[:, lanes:]

    def reduce_1(k):
        d_copy(k).wait_recv()
        for c in (chip_o, chip_r, chip_l, chip):
            for h in range(2):
                one = g_ref[k, piece(c, h)].astype(F32) + d_ref[k, 2 * c + h].astype(F32)
                g_ref[k, piece(c, h)] = one.astype(BF)
        for e in range(2):
            i_copy(k, e).start()
        for e in range(2):
            ii_copy(k, e).start()

    def reduce_2(k):
        for e in range(2):
            i_copy(k, e).wait_recv()
            one = g_ref[k, piece(toward[e], e)].astype(F32) + i_ref[k, e].astype(F32)
            i_ref[k, e] = one.astype(BF)
            iii_copy(k, e).start()

    def reduce_3(k):
        for e in range(2):
            ii_copy(k, e).wait_recv()
            iii_copy(k, e).wait_recv()
        for h in range(2):
            one = g_ref[k, piece(chip, h)].astype(F32) + q_ref[k, 0, h].astype(F32) + q_ref[k, 1, h].astype(F32)
            go[k, piece(chip, h)] = one.astype(BF)
        for e in range(2):
            ag1_copy(k, e, chip).start()
        p_copy(k, 0, chip, core).start()

    def gather_2(k):
        for e in range(2):
            ag1_copy(k, e, behind[e]).wait_recv()
            ag2_copy(k, e, behind[e]).start()
            p_copy(k, 1 + e, behind[e], core).start()

    def gather_3(k):
        for e in range(2):
            ag2_copy(k, e, chip_o).wait_recv()
        p_copy(k, 3, chip_o, core).start()

    def done_copy(k):
        return pltpu.make_async_copy(go.at[k], out.at[k], out_sem.at[k])

    def finish(k):
        for j, c in enumerate((chip, *behind, chip_o)):
            p_copy(k, j, c, 1 - core).wait_recv()
        done_copy(k).start()

    def when(condition):
        return pl.when(condition)

    def step(k, carry):
        @when(k < mats)
        def _():
            left_load(k, lax.rem(k, 2)).wait()

            @when(k + 1 < mats)
            def _():
                left_load(k + 1, lax.rem(k + 1, 2)).start()

            lax.fori_loop(0, chunks // 2, lambda c, _: multiply(k, c), None)
            d_copy(k).start()

        @when(k >= 1)
        def _():
            reduce_2(k - 1)

        @when(k < mats)
        def _():
            lax.fori_loop(chunks // 2, chunks, lambda c, _: multiply(k, c), None)
            reduce_1(k)

        @when(k >= 3)
        def _():
            gather_2(k - 3)

        @when(k >= 1)
        def _():
            reduce_3(k - 1)

        return carry

    lax.fori_loop(0, mats + 1, step, 0)
    lax.fori_loop(mats - 2, mats, lambda k, _: gather_2(k), None)
    lax.fori_loop(0, mats, lambda k, _: gather_3(k), None)
    lax.fori_loop(0, mats, lambda k, _: finish(k), None)

    def drain(k, carry):
        d_copy(k).wait_send()
        for e in range(2):
            i_copy(k, e).wait_send()
            ii_copy(k, e).wait_send()
            iii_copy(k, e).wait_send()
            ag1_copy(k, e, chip).wait_send()
            ag2_copy(k, e, behind[e]).wait_send()
        for j, c in enumerate((chip, *behind, chip_o)):
            p_copy(k, j, c, core).wait_send()
        done_copy(k).wait()
        return carry

    lax.fori_loop(0, mats, drain, 0)


def gradients(wide, turned, n):
    mats, chunks, tokens, chunk = wide.shape
    d = turned.shape[1]
    pieces = 2 * n
    lanes = chunks * chunk // pieces
    dma = lambda *shape: pltpu.SemaphoreType.DMA(shape)
    pairs = [dma(mats), dma(mats)] + [dma(mats, 2)] * 10 + [dma(mats, 4)] * 2
    return pl.pallas_call(
        functools.partial(sum_kernel, n),
        name="gradients",
        in_specs=[pl.BlockSpec(memory_space=pl.ANY)] * 2,
        out_specs=pl.BlockSpec(memory_space=pl.ANY),
        out_shape=jax.ShapeDtypeStruct((mats, pieces, d, lanes), BF),
        scratch_shapes=[
            pltpu.VMEM((mats, pieces, d, lanes), BF),
            pltpu.VMEM((mats, pieces // 2, d, lanes), BF),
            pltpu.VMEM((mats, 2, d, lanes), BF),
            pltpu.VMEM((mats, 2, 2, d, lanes), BF),
            pltpu.VMEM((mats, pieces, d, lanes), BF),
            pltpu.VMEM((2, d, tokens), BF),
            pltpu.VMEM((3, tokens, chunk), BF),
            dma(5),
            dma(mats),
            *pairs,
        ],
        compiler_params=pltpu.CompilerParams(collective_id=0, has_side_effects=True, vmem_limit_bytes=VMEM_LIMIT),
    )(wide, turned)


def adamw(w, m, v, g):
    m = 0.9 * m + 0.1 * g
    v = 0.95 * v + 0.05 * g * g
    step = m * lax.rsqrt(v + 1e-8) + 0.1 * w
    return (w - 0.02 * step).astype(BF), m, v


def update_kernel(blocks, g_ref, *refs):
    ins, outs = refs[:9], refs[9:]
    t = pl.program_id(0)
    count, lanes = g_ref.shape[1], g_ref.shape[-1]
    for a in range(3):

        @pl.when(t // blocks == a)
        def _():
            w, m, v = (ins[a + 3 * i] for i in range(3))
            for j in range(count):
                span = pl.ds(j * lanes, lanes)
                g = g_ref[0, j].astype(F32)
                if a == 2:
                    at = (0, span, slice(None))
                    g = g.T
                else:
                    at = (0, slice(None), span)
                nw, nm, nv = adamw(w[at].astype(F32), m[at], v[at], g)
                outs[a][at] = nw
                outs[a + 3][at] = nm
                outs[a + 6][at] = nv


def update(g, weights, m, v, per_layer=4):
    layers, d, ff = weights[0].shape
    blocks = layers * per_layer
    count = g.shape[1] // per_layer
    order = (1, 2, 0)

    def g_map(t):
        a, b = t // blocks, lax.rem(t, blocks)
        return (layers - 1 - b // per_layer) * 3 + lax.rem(a + 1, 3), lax.rem(b, per_layer), 0, 0

    def spec(a):
        def at(t):
            b = jnp.clip(t - a * blocks, 0, blocks - 1)
            layer, part = b // per_layer, lax.rem(b, per_layer)
            return (layer, part, 0) if a == 2 else (layer, 0, part)

        return pl.BlockSpec((1, ff // per_layer, d) if a == 2 else (1, d, ff // per_layer), at)

    specs = [spec(a) for a in range(3)] * 3
    arrays = (*weights, *m, *v)
    return pl.pallas_call(
        functools.partial(update_kernel, blocks),
        name="update",
        grid=(3 * blocks,),
        in_specs=[pl.BlockSpec((1, count, *g.shape[2:]), g_map), *specs],
        out_specs=specs,
        out_shape=[jax.ShapeDtypeStruct(x.shape, x.dtype) for x in arrays],
        compiler_params=pltpu.CompilerParams(dimension_semantics=("arbitrary",), vmem_limit_bytes=VMEM_LIMIT),
    )(g, *arrays)


def solution(mesh):
    n = mesh.shape["dp"]

    def step(x, dy, *arrays):
        weights, m, v = (arrays[i : i + 3] for i in (0, 3, 6))
        wide, turned = chain(x[0], dy[0], *weights)
        g = gradients(wide, turned, n)
        return tuple(update(g, weights, m, v))

    return jax.shard_map(
        step,
        mesh=mesh,
        in_specs=(P(("rep", "dp"), None, None),) * 2 + (P(None, None, None),) * 9,
        out_specs=(P("rep", None, None),) * 9,
        check_vma=False,
    )
```

time: 394 us -> 234 us (0.59); the launches traced: 387 us -> 234 us
  Pallas kernels: 0 us -> 233 us
  matrix products: 179 us -> 0 us
  waiting for transfers between devices: 139 us -> 0 us
  other arithmetic: 46.2 us -> 0 us
  between operations: 14.8 us -> 0.81 us
  local copies, waits for them, and re-layouts: 8.49 us -> 0 us
    pallas_call x0 -> x3, Pallas kernels: none -> 233 us  [the longest x1 120 us: gradients(): pl.pallas_call(functools.partial(sum_kernel, n), name='gradients', in_spe...]
    dot_general x15 -> x0, matrix products: 179 us -> none  [the longest x5 67 us: layer(): gate = jnp.dot(a, w['w_gate'], preferred_element_type=jnp.float32)]
    psum x1 -> x0, waiting for transfers between devices: 139 us -> none  [step(): summed[number] = [lax.psum(by_w[name], 'dp') for name in NAMES]]
    convert_element_type x2 -> x0, other arithmetic: 44.4 us -> none  [adamw(): return ((w - 0.02 * step).astype(jnp.bfloat16), m, v)]
    unnamed x40 -> x0, local copies, waits for them, and re-layouts: 8.49 us -> none
  transfers between devices with their start and end apart: 1 -> 0, of which waited for: 1 -> 0; matrix products, arithmetic and copies ran while one was open for 0% -> 0% of each run, Pallas kernels for 0% -> 0%
where the time goes in v1:
time: 234 us
  Pallas kernels  233 us (100%)
    pallas_call x1, Pallas kernels, gradients(): pl.pallas_call(functools.partial(sum_kernel, n), name='gradients', in_spe...  120 us
    pallas_call x1, Pallas kernels, chain(): pl.pallas_call(functools.partial(chain_kernel, chunk), name='chain', grid...  58.5 us
    pallas_call x1, Pallas kernels, update(): pl.pallas_call(functools.partial(update_kernel, blocks), name='update', g...  54.7 us

profile of v1, /device:TPU:112, one launch (start us, length us, event | category | flops | bytes accessed | tf_op | source)
XLA Modules:
  0.0 233.8 jit_solution(12555985062336711532)
XLA Ops:
  0.6 58.5 %chain.1 = (bf16[6,4,2048,512]{3,2,1,0:T(8,128)(2,1)}, bf16[4,512,2048]{2,1,0:T(8,128)(2,1)}) custom-call(bf16[2048,512]{1,0:T(8,128)(2,1)} %bitcast.2, bf16[2048,512]{1,0:T(8,128)(2,1)} %bitcast.3, bf16[2,512,2048]{2,1,0:T(8,128)(2,1)} %refs_0_.1, bf16[2,512,2048]{2,1,0:T(8,128)(2,1)} %refs_1_.1, bf16[2,2048,512]{2,1,0:T(8,128)(2,1)} %refs_2_.1), custom_call_target="tpu_custom_call" | custom-call | tf_op jit(solution)/shard_map/chain/pallas_call | solution.py:89
  59.1 119.8 %gradients.1.g_ref = bf16[6,16,512,128]{3,2,1,0:T(8,128)(2,1)} custom-call(bf16[6,4,2048,512]{3,2,1,0:T(8,128)(2,1)} %get-tuple-element.11.wide, bf16[4,512,2048]{2,1,0:T(8,128)(2,1)} %get-tuple-element.12.turned), custom_call_target="tpu_custom_call" | custom-call | tf_op jit(solution)/shard_map/gradients/pallas_call | solution.py:295
  178.9 54.7 %update.1 = (bf16[2,512,2048]{2,1,0:T(8,128)(2,1)}, bf16[2,512,2048]{2,1,0:T(8,128)(2,1)}, bf16[2,2048,512]{2,1,0:T(8,128)(2,1)}, f32[2,512,2048]{2,1,0:T(8,128)...) custom-call(bf16[6,16,512,128]{3,2,1,0:T(8,128)(2,1)} %gradients.1.g, ...), custom_call_target="tpu_custom_call" | custom-call | tf_op jit(solution)/shard_map/update/pallas_call | solution.py:367
